TPU v7x, 256 devices: a whole 4x4x8 slice. The times are simulated.
256 devices in a mesh: freq: 8 (over y, x_hi), rec: 32 (over x_lo, z, core).
Axes of the slice: x: 4 (x_hi: 2, x_lo: 2; x = x_hi * 2 + x_lo), y: 4, z: 8, core: 2. Of those that a mesh axis runs over, the one named last changes fastest.
Arguments:
- response: bfloat16 [128, 2, 1792, 1792], P('freq', None, 'rec'), may hold values from -1 to 1, as said below
- direct: float32 [1792, 32, 256], P('rec', 'freq'), may hold values from -6 to 6
- onset: int32 [1792, 32], P('rec', 'freq'), may hold values from 16 to 128
Outputs:
- upgoing: float32 [1792, 32, 256], P('rec', 'freq')
- coda: float32 [1792, 32, 256], P('rec', 'freq')
Inputs may be any that keep to these rules, and one draw needn't show every extreme that they name: response[k, c, r, s] = response[k, c, s, r] for every frequency and part (source-receiver reciprocity).
All inputs are finite; a program needn't handle non-finite values.
Results may differ from a plain program's by a relative error of at most 0.023.
Values may be sent and summed in bfloat16 or wider, within the bound.
A program may use at most 128 MiB of HBM per device.

v0:
```python
import math
import jax
import jax.numpy as jnp
from jax import lax
from jax.sharding import PartitionSpec as P

NF = 128
NT = 256
ITERS = 2


def spectral_tables(length, count):
    samples = jnp.arange(length, dtype=jnp.int32)
    frequency_bins = jnp.arange(1, count + 1, dtype=jnp.int32)
    phase = (samples[:, None] * frequency_bins[None, :] % length).astype(jnp.float32) * (
        2.0 * math.pi / length
    )
    cosine = jnp.cos(phase)
    sine = jnp.sin(phase)
    forward = jnp.stack([cosine, -sine], axis=1)
    inverse = jnp.stack([cosine.T, -sine.T], axis=0) * (2.0 / length)
    return (forward, inverse)


def make_window(onset, length):
    samples = jnp.arange(length, dtype=jnp.int32)
    folded = jnp.minimum(samples, length - samples)
    return (folded[None, None, :] < onset[:, :, None]).astype(jnp.float32)


def to_spectrum(field, forward):
    packed = jnp.einsum("svt,tck->kcvs", field, forward)
    return packed.astype(jnp.bfloat16)


def to_time(spectra, inverse):
    return jnp.einsum("kcvs,ckt->svt", spectra.astype(jnp.float32), inverse)


def complex_apply(block, spectra, conj_sign):
    parts = jnp.einsum("fcrs,fdvs->cdfvr", block, spectra, preferred_element_type=jnp.float32)
    real_out = parts[0, 0] - conj_sign * parts[1, 1]
    imag_out = parts[0, 1] + conj_sign * parts[1, 0]
    return jnp.stack([real_out, imag_out], axis=1)


def body(response, direct, onset):
    forward, inverse = spectral_tables(NT, NF)
    window = make_window(onset, NT)
    coda = jnp.zeros_like(direct)
    upgoing = coda
    for iteration in range(ITERS):
        downgoing = direct + coda
        sources = lax.all_to_all(
            to_spectrum(downgoing, forward), "freq", split_axis=0, concat_axis=2, tiled=True
        )
        gathered = lax.all_gather(sources, "rec", axis=3, tiled=True)
        reflected = complex_apply(response, gathered, 1.0)
        reflected_time = lax.all_to_all(
            reflected.astype(jnp.bfloat16), "freq", split_axis=2, concat_axis=0, tiled=True
        )
        upgoing = window * to_time(reflected_time, inverse)
        spectra_up = lax.all_to_all(
            to_spectrum(upgoing, forward), "freq", split_axis=0, concat_axis=2, tiled=True
        )
        receivers = lax.all_gather(spectra_up, "rec", axis=3, tiled=True)
        returned = complex_apply(response, receivers, -1.0)
        returned_time = lax.all_to_all(
            returned.astype(jnp.bfloat16), "freq", split_axis=2, concat_axis=0, tiled=True
        )
        coda = window * to_time(returned_time, inverse)
    return (upgoing, coda)


def solution(mesh):
    placed = (P("freq", None, "rec", None), P("rec", "freq", None), P("rec", "freq"))
    return jax.shard_map(
        body,
        mesh=mesh,
        in_specs=placed,
        out_specs=(P("rec", "freq", None), P("rec", "freq", None)),
        check_vma=False,
    )
```

profile of v0, /device:TPU:96, one launch (start us, length us, event | category | flops | bytes accessed | tf_op | source)
XLA Modules:
  0.0 545.7 jit_solution(14085154062390279766)
XLA Ops:
  7.2 0.5 fusion.96
  7.8 1.1 fusion.39
  8.9 0.2 copy.86
  9.1 0.4 reshape.396
  9.5 14.9 %all_to_all.144 = bf16[8,2,3584]{2,1,0:T(2,128)(2,1)S(1)} all-to-all(bf16[8,2,3584]{2,1,0:T(2,128)(2,1)S(1)} %reshape.396), channel_id=1, replica_groups=mesh['freq'=8,'rec'=32] {'freq'}, dimensions={0} | all-to-all | bytes 229376 | tf_op jit(solution)/shard_map/all_to_all | solution.py:54
  24.4 0.4 reshape.397
  24.9 1.5 copy.89
  26.4 0.6 fusion.97
  27.0 87.4 %all-gather.5.cloned.1.call-done = bf16[16,2,32,1792]{2,0,1,3:T(8,128)(2,1)} async-done(((bf16[16,2,32,56]{2,0,1,3:T(8,128)(2,1)}), bf16[16,2,32,1792]{2,0,1,3:T(8,128)(2,1)}) %all-gather.5.cloned.1.call-update) | async-done | bytes 3670032 | tf_op jit(solution)/shard_map/all_gather | solution.py:57
  114.4 15.0 %fusion.17 = f32[2,2,16,32,56]{4,3,0,1,2:T(8,128)S(1)} fusion(bf16[16,2,56,1792]{3,2,1,0:T(8,128)(2,1)} %param.3, bf16[16,2,32,1792,1]{2,0,1,3,4:T(8,128)(2,1)} %bitcast.271), kind=kOutput, calls=%fused_computation.13 | convolution fusion | flops 411041792 | bytes 10551296 | tf_op jit(solution)/shard_map/fcrs,fdvs->cdfvr/dot_general | solution.py:41
  129.5 0.1 fusion.77
  129.6 0.1 pad_maximum_fusion
  129.6 0.1 copy.198
  129.7 1.1 reshape.398
  130.8 6.7 %all-to-all-start.1 = ((bf16[8,2,3584]{2,1,0:T(2,128)(2,1)}), bf16[8,2,3584]{2,1,0:T(2,128)(2,1)S(1)}, u32[]{:S(2)}, u32[]{:S(2)}) async-start(bf16[8,2,3584]{2,1,0:T(2,128)(2,1)} %reshape.398), calls=%async_computation.1 | async-start | bytes 229376 | tf_op jit(solution)/shard_map/all_to_all | solution.py:59
  137.6 8.1 %all-to-all-done.1 = bf16[8,2,3584]{2,1,0:T(2,128)(2,1)S(1)} async-done(((bf16[8,2,3584]{2,1,0:T(2,128)(2,1)}), bf16[8,2,3584]{2,1,0:T(2,128)(2,1)S(1)}, u32[]{:S(2)}, u32[]{:S(2)}) %all-to-all-start.1) | async-done | bytes 114720 | tf_op jit(solution)/shard_map/all_to_all | solution.py:59
  145.6 0.4 reshape.399
  146.1 0.4 fusion.40
  146.5 0.2 copy.96
  146.7 0.4 reshape.400
  147.1 10.5 %all_to_all.145 = bf16[8,2,3584]{2,1,0:T(2,128)(2,1)S(1)} all-to-all(bf16[8,2,3584]{2,1,0:T(2,128)(2,1)S(1)} %reshape.400), channel_id=1, replica_groups=mesh['freq'=8,'rec'=32] {'freq'}, dimensions={0} | all-to-all | bytes 229376 | tf_op jit(solution)/shard_map/all_to_all | solution.py:63
  157.6 0.4 reshape.401
  158.2 1.5 copy.99
  159.6 0.2 all-gather.9.cloned.1.call-start
  159.9 85.8 %all-gather.7.cloned.1.call-done = bf16[16,2,32,1792]{2,0,1,3:T(8,128)(2,1)} async-done(((bf16[16,2,32,56]{2,0,1,3:T(8,128)(2,1)}), bf16[16,2,32,1792]{2,0,1,3:T(8,128)(2,1)}) %all-gather.7.cloned.1.call-update) | async-done | bytes 3670032 | tf_op jit(solution)/shard_map/all_gather | solution.py:66
  245.6 15.1 %fusion.22 = f32[2,2,16,32,56]{4,3,0,1,2:T(8,128)S(1)} fusion(bf16[16,2,56,1792]{3,2,1,0:T(8,128)(2,1)} %param.3, bf16[16,2,32,1792,1]{2,0,1,3,4:T(8,128)(2,1)} %bitcast.272), kind=kOutput, calls=%fused_computation.14 | convolution fusion | flops 411041792 | bytes 10551296 | tf_op jit(solution)/shard_map/fcrs,fdvs->cdfvr/dot_general | solution.py:41
  260.7 0.1 fusion.79
  260.9 0.1 copy.197
  261.0 0.4 reshape.402
  261.4 14.6 %all_to_all.146 = bf16[8,2,3584]{2,1,0:T(2,128)(2,1)S(1)} all-to-all(bf16[8,2,3584]{2,1,0:T(2,128)(2,1)S(1)} %reshape.402), channel_id=1, replica_groups=mesh['freq'=8,'rec'=32] {'freq'}, dimensions={0} | all-to-all | bytes 229376 | tf_op jit(solution)/shard_map/all_to_all | solution.py:68
  276.1 0.4 reshape.403
  276.5 0.4 fusion.41
  276.9 0.2 copy.108
  277.1 0.4 reshape.404
  277.5 10.5 %all_to_all.147 = bf16[8,2,3584]{2,1,0:T(2,128)(2,1)S(1)} all-to-all(bf16[8,2,3584]{2,1,0:T(2,128)(2,1)S(1)} %reshape.404), channel_id=1, replica_groups=mesh['freq'=8,'rec'=32] {'freq'}, dimensions={0} | all-to-all | bytes 229376 | tf_op jit(solution)/shard_map/all_to_all | solution.py:54
  288.1 0.4 reshape.405
  288.6 1.5 copy.111
  290.1 0.3 all-gather.11.cloned.1.call-start
  290.3 85.7 %all-gather.9.cloned.1.call-done = bf16[16,2,32,1792]{2,0,1,3:T(8,128)(2,1)} async-done(((bf16[16,2,32,56]{2,0,1,3:T(8,128)(2,1)}), bf16[16,2,32,1792]{2,0,1,3:T(8,128)(2,1)}) %all-gather.9.cloned.1.call-update) | async-done | bytes 3670032 | tf_op jit(solution)/shard_map/all_gather | solution.py:57
  376.0 15.0 %fusion.27 = f32[2,2,16,32,56]{4,3,0,1,2:T(8,128)S(1)} fusion(bf16[16,2,56,1792]{3,2,1,0:T(8,128)(2,1)} %param.3, bf16[16,2,32,1792,1]{2,0,1,3,4:T(8,128)(2,1)} %bitcast.273), kind=kOutput, calls=%fused_computation.15 | convolution fusion | flops 411041792 | bytes 10551296 | tf_op jit(solution)/shard_map/fcrs,fdvs->cdfvr/dot_general | solution.py:41
  391.1 0.1 fusion.81
  391.2 0.1 copy.196
  391.3 0.4 reshape.406
  391.8 14.6 %all_to_all.148 = bf16[8,2,3584]{2,1,0:T(2,128)(2,1)S(1)} all-to-all(bf16[8,2,3584]{2,1,0:T(2,128)(2,1)S(1)} %reshape.406), channel_id=1, replica_groups=mesh['freq'=8,'rec'=32] {'freq'}, dimensions={0} | all-to-all | bytes 229376 | tf_op jit(solution)/shard_map/all_to_all | solution.py:59
  406.4 0.4 reshape.407
  406.9 0.2 fusion.37
  407.1 0.2 fusion.42
  407.3 0.2 copy.118
  407.5 0.4 reshape.408
  407.9 10.5 %all_to_all.149 = bf16[8,2,3584]{2,1,0:T(2,128)(2,1)S(1)} all-to-all(bf16[8,2,3584]{2,1,0:T(2,128)(2,1)S(1)} %reshape.408), channel_id=1, replica_groups=mesh['freq'=8,'rec'=32] {'freq'}, dimensions={0} | all-to-all | bytes 229376 | tf_op jit(solution)/shard_map/all_to_all | solution.py:63
  418.5 0.4 reshape.409
  419.0 1.5 copy.121
  420.5 86.0 %all-gather.11.cloned.1.call-done = bf16[16,2,32,1792]{2,0,1,3:T(8,128)(2,1)} async-done(((bf16[16,2,32,56]{2,0,1,3:T(8,128)(2,1)}), bf16[16,2,32,1792]{2,0,1,3:T(8,128)(2,1)}) %all-gather.11.cloned.1.call-update) | async-done | bytes 3670032 | tf_op jit(solution)/shard_map/all_gather | solution.py:66
  506.5 15.0 %fusion.12 = f32[2,2,16,32,56]{4,3,2,1,0:T(8,128)S(1)} fusion(bf16[16,2,32,1792,1]{2,0,1,3,4:T(8,128)(2,1)} %bitcast.274, bf16[16,2,56,1792]{3,2,1,0:T(8,128)(2,1)} %param.3), kind=kOutput, calls=%fused_computation.12 | convolution fusion | flops 411041792 | bytes 10551296 | tf_op jit(solution)/shard_map/fcrs,fdvs->cdfvr/dot_general | solution.py:41
  521.5 0.1 fusion.82
  521.6 0.1 pad_maximum_fusion.3
  521.7 0.1 copy.195
  521.8 1.1 reshape.410
  522.8 6.7 %all-to-all-start.7 = ((bf16[8,2,3584]{2,1,0:T(2,128)(2,1)}), bf16[8,2,3584]{2,1,0:T(2,128)(2,1)S(1)}, u32[]{:S(2)}, u32[]{:S(2)}) async-start(bf16[8,2,3584]{2,1,0:T(2,128)(2,1)} %reshape.410), calls=%async_computation.7 | async-start | bytes 229376 | tf_op jit(solution)/shard_map/all_to_all | solution.py:68
  529.5 0.8 copy.127
  530.3 7.4 %all-to-all-done.7 = bf16[8,2,3584]{2,1,0:T(2,128)(2,1)S(1)} async-done(((bf16[8,2,3584]{2,1,0:T(2,128)(2,1)}), bf16[8,2,3584]{2,1,0:T(2,128)(2,1)S(1)}, u32[]{:S(2)}, u32[]{:S(2)}) %all-to-all-start.7) | async-done | bytes 114720 | tf_op jit(solution)/shard_map/all_to_all | solution.py:68
  537.7 0.4 reshape.411
  538.2 0.2 fusion.38
  538.4 0.8 copy.128
  (29 shorter events, 0.7 us)
Async XLA Ops:
  7.2 107.3 %all-gather.5.cloned.1.call-start = ((), (), s32[]{:S(2)}) async-start(), calls=%async_computation.8 | async-start | bytes 15138816 | tf_op jit(solution)/shard_map/all_gather | solution.py:57
  114.4 31.7 %copy-start.1 = (s32[56,4]{0,1:T(4,128)S(1)}, s32[56,4]{0,1:T(4,128)}, u32[]{:S(2)}) copy-start(s32[56,4]{0,1:T(4,128)} %param.5) | copy-start | bytes 2692
  130.8 14.8 %all-to-all-start.1 = ((bf16[8,2,3584]{2,1,0:T(2,128)(2,1)}), bf16[8,2,3584]{2,1,0:T(2,128)(2,1)S(1)}, u32[]{:S(2)}, u32[]{:S(2)}) async-start(bf16[8,2,3584]{2,1,0:T(2,128)(2,1)} %reshape.398), calls=%async_computation.1 | async-start | bytes 229376 | tf_op jit(solution)/shard_map/all_to_all | solution.py:59
  137.5 108.1 %all-gather.7.cloned.1.call-start = ((), (), s32[]{:S(2)}) async-start(), calls=%async_computation.9 | async-start | bytes 15138816 | tf_op jit(solution)/shard_map/all_gather | solution.py:66
  159.6 216.4 %all-gather.9.cloned.1.call-start = ((), (), s32[]{:S(2)}) async-start(), calls=%async_computation.10 | async-start | bytes 15138816 | tf_op jit(solution)/shard_map/all_gather | solution.py:57
  245.6 30.9 %copy-start = (f32[56,4,256]{2,1,0:T(4,128)S(1)}, f32[56,4,256]{2,1,0:T(4,128)}, u32[]{:S(2)}) copy-start(f32[56,4,256]{2,1,0:T(4,128)} %param.4) | copy-start | bytes 688132
  290.1 216.4 %all-gather.11.cloned.1.call-start = ((), (), s32[]{:S(2)}) async-start(), calls=%async_computation.11 | async-start | bytes 15138816 | tf_op jit(solution)/shard_map/all_gather | solution.py:66
  522.8 14.8 %all-to-all-start.7 = ((bf16[8,2,3584]{2,1,0:T(2,128)(2,1)}), bf16[8,2,3584]{2,1,0:T(2,128)(2,1)S(1)}, u32[]{:S(2)}, u32[]{:S(2)}) async-start(bf16[8,2,3584]{2,1,0:T(2,128)(2,1)} %reshape.410), calls=%async_computation.7 | async-start | bytes 229376 | tf_op jit(solution)/shard_map/all_to_all | solution.py:68
Sparse Core Ops, SparseCore 0:
  26.5 87.8 all-gather.4
  159.8 85.8 all-gather.6
  290.2 85.8 all-gather.8
  420.6 85.8 all-gather.10
where the time goes:
time: 546 us
  waiting for transfers between devices  360 us (66%)
  blocking collectives  75.7 us (14%)
  matrix products  62.6 us (11%)
  local copies, waits for them, and re-layouts  17 us (3%)
  between operations  14.2 us (3%)
  starting transfers between devices  14 us (3%)
    all_gather x2, waiting for transfers between devices, body(): gathered = lax.all_gather(sources, 'rec', axis=3, tiled=True)  173 us
    all_gather x2, waiting for transfers between devices, body(): receivers = lax.all_gather(spectra_up, 'rec', axis=3, tiled=True)  172 us
    dot_general x4, matrix products, complex_apply(): jnp.einsum('fcrs,fdvs->cdfvr', block, spectra, preferred_element_type=jnp...  60.1 us
    all_to_all x2, blocking collectives, body(): lax.all_to_all(to_spectrum(downgoing, forward), 'freq', split_axis=0, con...  25.4 us
    all_to_all x2, blocking collectives, body(): lax.all_to_all(to_spectrum(upgoing, forward), 'freq', split_axis=0, conca...  21.1 us
    all_to_all x1, blocking collectives, body(): lax.all_to_all(reflected.astype(jnp.bfloat16), 'freq', split_axis=2, conc...  14.6 us
    all_to_all x1, blocking collectives, body(): lax.all_to_all(returned.astype(jnp.bfloat16), 'freq', split_axis=2, conca...  14.6 us
  transfers between devices with their start and end apart: 6, of which 6 were waited for; matrix products, arithmetic and copies ran while one was open for 0% of the time, Pallas kernels for 0%

commit v1 on v0

--- a/solution.py
+++ b/solution.py
@@ -1,3 +1,4 @@
+import functools
 import math
 import jax
 import jax.numpy as jnp
@@ -7,6 +8,15 @@
 NF = 128
 NT = 256
 ITERS = 2
+
+
+def load_column(z_in, net_axis):
+    return jnp.concatenate(
+        lax.all_to_all(jnp.stack([z_in] * lax.axis_size(net_axis), axis=0), net_axis, 0, 0), 3
+    )
+
+
+counts_assign = functools.partial(load_column, net_axis="rec")
 
 
 def spectral_tables(length, count):
@@ -54,7 +64,7 @@
         sources = lax.all_to_all(
             to_spectrum(downgoing, forward), "freq", split_axis=0, concat_axis=2, tiled=True
         )
-        gathered = lax.all_gather(sources, "rec", axis=3, tiled=True)
+        gathered = counts_assign(sources)
         reflected = complex_apply(response, gathered, 1.0)
         reflected_time = lax.all_to_all(
             reflected.astype(jnp.bfloat16), "freq", split_axis=2, concat_axis=0, tiled=True

time: 546 us -> 698 us (1.28); the launches traced: 546 us -> 690 us
  local copies, waits for them, and re-layouts: 17 us -> 176 us
  waiting for transfers between devices: 360 us -> 271 us
  blocking collectives: 75.7 us -> 161 us
  matrix products: 62.6 us -> 47.6 us
    all_gather x2 -> x0, waiting for transfers between devices: 173 us -> none  [body(): gathered = lax.all_gather(sources, 'rec', axis=3, tiled=True)]
    all_to_all x0 -> x1, blocking collectives: none -> 88.9 us  [load_column(): lax.all_to_all(jnp.stack([z_in] * lax.axis_size(net_axis), axis=0), net_a...]
    all_to_all x0 -> x1, waiting for transfers between devices: none -> 84.2 us  [load_column(): lax.all_to_all(jnp.stack([z_in] * lax.axis_size(net_axis), axis=0), net_a...]
    unnamed x22 -> x26, local copies, waits for them, and re-layouts: 9.64 us -> 91.8 us
    reshape x0 -> x4, local copies, waits for them, and re-layouts: none -> 68.5 us  [load_column(): jnp.concatenate(lax.all_to_all(jnp.stack([z_in] * lax.axis_size(net_axis)...]
    dot_general x4, matrix products: 60.1 us -> 45.1 us  [complex_apply(): jnp.einsum('fcrs,fdvs->cdfvr', block, spectra, preferred_element_type=jnp...]
    another operation x0 -> x4, local copies, waits for them, and re-layouts: none -> 10.9 us  [load_column(): jnp.stack([z_in] * lax.axis_size(net_axis), axis=0)]
    all_to_all x0 -> x1, starting transfers between devices: none -> 7.9 us  [load_column(): lax.all_to_all(jnp.stack([z_in] * lax.axis_size(net_axis), axis=0), net_a...]
  transfers between devices with their start and end apart: 6 -> 5, of which waited for: 6 -> 5; matrix products, arithmetic and copies ran while one was open for 0% -> 0% of each run, Pallas kernels for 0% -> 0%
where the time goes in v1:
time: 698 us; the launch traced here: 690 us
  waiting for transfers between devices  271 us (39%)
  local copies, waits for them, and re-layouts  176 us (25%)
  blocking collectives  161 us (23%)
  matrix products  47.6 us (7%)
  starting transfers between devices  18 us (3%)
  between operations  14.7 us (2%)
    all_gather x2, waiting for transfers between devices, body(): receivers = lax.all_gather(spectra_up, 'rec', axis=3, tiled=True)  172 us
    unnamed x26, local copies, waits for them, and re-layouts  91.8 us
    all_to_all x1, blocking collectives, load_column(): lax.all_to_all(jnp.stack([z_in] * lax.axis_size(net_axis), axis=0), net_a...  88.9 us
    all_to_all x1, waiting for transfers between devices, load_column(): lax.all_to_all(jnp.stack([z_in] * lax.axis_size(net_axis), axis=0), net_a...  84.2 us
    reshape x4, local copies, waits for them, and re-layouts, load_column(): jnp.concatenate(lax.all_to_all(jnp.stack([z_in] * lax.axis_size(net_axis)...  68.5 us
    dot_general x4, matrix products, complex_apply(): jnp.einsum('fcrs,fdvs->cdfvr', block, spectra, preferred_element_type=jnp...  45.1 us
    all_to_all x2, blocking collectives, body(): lax.all_to_all(to_spectrum(downgoing, forward), 'freq', split_axis=0, con...  25.4 us
    all_to_all x2, blocking collectives, body(): lax.all_to_all(to_spectrum(upgoing, forward), 'freq', split_axis=0, conca...  21.2 us
  transfers between devices with their start and end apart: 5, of which 5 were waited for; matrix products, arithmetic and copies ran while one was open for 0% of the time, Pallas kernels for 0%

profile of v1, /device:TPU:96, one launch (start us, length us, event | category | flops | bytes accessed | tf_op | source)
XLA Modules:
  0.0 689.6 jit_solution(9815836827543083634)
XLA Ops:
  7.2 0.5 fusion.96
  7.7 1.1 fusion.39
  8.9 0.2 copy.90
  9.1 0.4 reshape.420
  9.5 14.9 %all_to_all.148 = bf16[8,2,3584]{2,1,0:T(2,128)(2,1)S(1)} all-to-all(bf16[8,2,3584]{2,1,0:T(2,128)(2,1)S(1)} %reshape.420), channel_id=1, replica_groups=mesh['freq'=8,'rec'=32] {'freq'}, dimensions={0} | all-to-all | bytes 229376 | tf_op jit(solution)/shard_map/all_to_all | solution.py:64
  24.3 0.4 reshape.421
  24.9 5.4 stack.27
  30.3 19.8 %reshape.422 = bf16[32,2,28672]{2,1,0:T(2,128)(2,1)} reshape(bf16[32,16,2,32,56]{4,3,2,1,0:T(8,128)(2,1)} %stack.27) | data formatting | bytes 7340032
  50.1 7.9 %all-to-all-start.1 = ((bf16[32,2,28672]{2,1,0:T(2,128)(2,1)}), bf16[32,2,28672]{2,1,0:T(2,128)(2,1)}, u32[]{:S(2)}, u32[]{:S(2)}) async-start(bf16[32,2,28672]{2,1,0:T(2,128)(2,1)} %reshape.422), calls=%async_computation.1 | async-start | bytes 7340032 | tf_op jit(solution)/shard_map/all_to_all | solution.py:15
  58.0 0.6 fusion.97
  58.6 84.2 %all-to-all-done.1 = bf16[32,2,28672]{2,1,0:T(2,128)(2,1)} async-done(((bf16[32,2,28672]{2,1,0:T(2,128)(2,1)}), bf16[32,2,28672]{2,1,0:T(2,128)(2,1)}, u32[]{:S(2)}, u32[]{:S(2)}) %all-to-all-start.1) | async-done | bytes 3670048 | tf_op jit(solution)/shard_map/all_to_all | solution.py:15
  142.8 21.3 %reshape.423 = bf16[32,16,2,32,56]{4,3,2,1,0:T(8,128)(2,1)} reshape(bf16[32,2,28672]{2,1,0:T(2,128)(2,1)} %all-to-all-done.1) | data formatting | bytes 7340032
  164.1 20.0 %copy.94 = bf16[16,2,32,32,56]{4,3,2,1,0:T(8,128)(2,1)} copy(bf16[16,2,32,32,56]{4,2,1,0,3:T(8,128)(2,1)} %bitcast.265) | data formatting | bytes 7340032 | tf_op jit(solution)/shard_map/reshape | solution.py:14
  184.1 14.3 %reshape.405 = bf16[16,2,32,1792,1]{3,2,1,0,4:T(8,128)(2,1)} reshape(bf16[16,2,32,32,56]{4,3,2,1,0:T(8,128)(2,1)} %copy.94) | data formatting | bytes 7340032 | tf_op jit(solution)/shard_map/reshape | solution.py:14
  198.3 7.4 %fusion.17 = f32[2,2,16,32,56]{4,3,0,1,2:T(8,128)S(1)} fusion(bf16[16,2,56,1792]{3,2,1,0:T(8,128)(2,1)} %param.3, bf16[16,2,32,1792,1]{3,2,1,0,4:T(8,128)(2,1)} %reshape.405), kind=kOutput, calls=%fused_computation.13 | convolution fusion | flops 411041792 | bytes 10551296 | tf_op jit(solution)/shard_map/fcrs,fdvs->cdfvr/dot_general | solution.py:51
  205.9 0.1 copy.190
  206.0 1.1 reshape.424
  207.0 3.4 all-to-all-start.2
  210.5 8.0 %all-to-all-done.2 = bf16[8,2,3584]{2,1,0:T(2,128)(2,1)S(1)} async-done(((bf16[8,2,3584]{2,1,0:T(2,128)(2,1)}), bf16[8,2,3584]{2,1,0:T(2,128)(2,1)S(1)}, u32[]{:S(2)}, u32[]{:S(2)}) %all-to-all-start.2) | async-done | bytes 114720 | tf_op jit(solution)/shard_map/all_to_all | solution.py:69
  218.5 0.4 reshape.425
  218.9 0.4 fusion.40
  219.3 0.2 copy.100
  219.5 0.4 reshape.426
  219.9 10.5 %all_to_all.149 = bf16[8,2,3584]{2,1,0:T(2,128)(2,1)S(1)} all-to-all(bf16[8,2,3584]{2,1,0:T(2,128)(2,1)S(1)} %reshape.426), channel_id=1, replica_groups=mesh['freq'=8,'rec'=32] {'freq'}, dimensions={0} | all-to-all | bytes 229376 | tf_op jit(solution)/shard_map/all_to_all | solution.py:73
  230.5 0.4 reshape.427
  231.0 1.4 copy.103
  232.5 85.8 %all-gather.3.cloned.1.call-done = bf16[16,2,32,1792]{2,0,1,3:T(8,128)(2,1)} async-done(((bf16[16,2,32,56]{2,0,1,3:T(8,128)(2,1)}), bf16[16,2,32,1792]{2,0,1,3:T(8,128)(2,1)}) %all-gather.3.cloned.1.call-update) | async-done | bytes 3670032 | tf_op jit(solution)/shard_map/all_gather | solution.py:76
  318.3 15.3 %fusion.27 = f32[2,2,16,32,56]{4,3,0,1,2:T(8,128)S(1)} fusion(bf16[16,2,56,1792]{3,2,1,0:T(8,128)(2,1)} %param.3, bf16[16,2,32,1792,1]{2,0,1,3,4:T(8,128)(2,1)} %bitcast.287), kind=kOutput, calls=%fused_computation.15 | convolution fusion | flops 411041792 | bytes 10551296 | tf_op jit(solution)/shard_map/fcrs,fdvs->cdfvr/dot_general | solution.py:51
  333.7 0.1 copy.189
  333.8 0.4 reshape.428
  334.3 14.6 %all_to_all.150 = bf16[8,2,3584]{2,1,0:T(2,128)(2,1)S(1)} all-to-all(bf16[8,2,3584]{2,1,0:T(2,128)(2,1)S(1)} %reshape.428), channel_id=1, replica_groups=mesh['freq'=8,'rec'=32] {'freq'}, dimensions={0} | all-to-all | bytes 229376 | tf_op jit(solution)/shard_map/all_to_all | solution.py:78
  348.9 0.4 reshape.429
  349.4 0.4 fusion.41
  349.7 0.2 copy.112
  349.9 0.4 reshape.430
  350.4 10.5 %all_to_all.151 = bf16[8,2,3584]{2,1,0:T(2,128)(2,1)S(1)} all-to-all(bf16[8,2,3584]{2,1,0:T(2,128)(2,1)S(1)} %reshape.430), channel_id=1, replica_groups=mesh['freq'=8,'rec'=32] {'freq'}, dimensions={0} | all-to-all | bytes 229376 | tf_op jit(solution)/shard_map/all_to_all | solution.py:64
  360.9 0.4 reshape.431
  361.5 5.4 stack.31
  366.9 19.8 %reshape.432 = bf16[32,2,28672]{2,1,0:T(2,128)(2,1)} reshape(bf16[32,16,2,32,56]{4,3,2,1,0:T(8,128)(2,1)} %stack.31) | data formatting | bytes 7340032
  386.7 88.9 %all_to_all.152 = bf16[32,2,28672]{2,1,0:T(2,128)(2,1)} all-to-all(bf16[32,2,28672]{2,1,0:T(2,128)(2,1)} %reshape.432), channel_id=1, replica_groups=mesh['freq'=8,'rec'=32] {'rec'}, dimensions={0} | all-to-all | bytes 7340032 | tf_op jit(solution)/shard_map/all_to_all | solution.py:15
  475.6 21.2 %reshape.433 = bf16[32,16,2,32,56]{4,3,2,1,0:T(8,128)(2,1)} reshape(bf16[32,2,28672]{2,1,0:T(2,128)(2,1)} %all_to_all.152) | data formatting | bytes 7340032
  496.8 20.0 %copy.116 = bf16[16,2,32,32,56]{4,3,2,1,0:T(8,128)(2,1)} copy(bf16[16,2,32,32,56]{4,2,1,0,3:T(8,128)(2,1)} %bitcast.266) | data formatting | bytes 7340032 | tf_op jit(solution)/shard_map/reshape | solution.py:14
  516.8 14.3 %reshape.413 = bf16[16,2,32,1792,1]{3,2,1,0,4:T(8,128)(2,1)} reshape(bf16[16,2,32,32,56]{4,3,2,1,0:T(8,128)(2,1)} %copy.116) | data formatting | bytes 7340032 | tf_op jit(solution)/shard_map/reshape | solution.py:14
  531.0 7.4 %fusion.22 = f32[2,2,16,32,56]{4,3,0,1,2:T(8,128)S(1)} fusion(bf16[16,2,56,1792]{3,2,1,0:T(8,128)(2,1)} %param.3, bf16[16,2,32,1792,1]{3,2,1,0,4:T(8,128)(2,1)} %reshape.413), kind=kOutput, calls=%fused_computation.14 | convolution fusion | flops 411041792 | bytes 10551296 | tf_op jit(solution)/shard_map/fcrs,fdvs->cdfvr/dot_general | solution.py:51
  538.7 0.4 reshape.434
  539.1 10.6 %all_to_all.153 = bf16[8,2,3584]{2,1,0:T(2,128)(2,1)S(1)} all-to-all(bf16[8,2,3584]{2,1,0:T(2,128)(2,1)S(1)} %reshape.434), channel_id=1, replica_groups=mesh['freq'=8,'rec'=32] {'freq'}, dimensions={0} | all-to-all | bytes 229376 | tf_op jit(solution)/shard_map/all_to_all | solution.py:69
  549.7 0.4 reshape.435
  550.2 0.2 fusion.37
  550.5 0.2 fusion.42
  550.6 0.2 copy.122
  550.8 0.4 reshape.436
  551.3 10.7 %all_to_all.154 = bf16[8,2,3584]{2,1,0:T(2,128)(2,1)S(1)} all-to-all(bf16[8,2,3584]{2,1,0:T(2,128)(2,1)S(1)} %reshape.436), channel_id=1, replica_groups=mesh['freq'=8,'rec'=32] {'freq'}, dimensions={0} | all-to-all | bytes 229376 | tf_op jit(solution)/shard_map/all_to_all | solution.py:73
  562.0 0.4 reshape.437
  562.5 1.4 copy.125
  564.0 85.8 %all-gather.5.cloned.1.call-done = bf16[16,2,32,1792]{2,0,1,3:T(8,128)(2,1)} async-done(((bf16[16,2,32,56]{2,0,1,3:T(8,128)(2,1)}), bf16[16,2,32,1792]{2,0,1,3:T(8,128)(2,1)}) %all-gather.5.cloned.1.call-update) | async-done | bytes 3670032 | tf_op jit(solution)/shard_map/all_gather | solution.py:76
  649.8 15.1 %fusion.12 = f32[2,2,16,32,56]{4,3,2,1,0:T(8,128)S(1)} fusion(bf16[16,2,32,1792,1]{2,0,1,3,4:T(8,128)(2,1)} %bitcast.288, bf16[16,2,56,1792]{3,2,1,0:T(8,128)(2,1)} %param.3), kind=kOutput, calls=%fused_computation.12 | convolution fusion | flops 411041792 | bytes 10551296 | tf_op jit(solution)/shard_map/fcrs,fdvs->cdfvr/dot_general | solution.py:51
  664.9 0.1 fusion.82
  665.2 1.1 reshape.438
  666.2 6.7 all-to-all-start.9
  672.9 0.8 copy.131
  673.7 7.4 %all-to-all-done.9 = bf16[8,2,3584]{2,1,0:T(2,128)(2,1)S(1)} async-done(((bf16[8,2,3584]{2,1,0:T(2,128)(2,1)}), bf16[8,2,3584]{2,1,0:T(2,128)(2,1)S(1)}, u32[]{:S(2)}, u32[]{:S(2)}) %all-to-all-start.9) | async-done | bytes 114720 | tf_op jit(solution)/shard_map/all_to_all | solution.py:78
  681.1 0.4 reshape.439
  681.5 0.2 fusion.38
  681.8 0.8 copy.132
  (36 shorter events, 1.3 us)
Async XLA Ops:
  50.1 92.7 %all-to-all-start.1 = ((bf16[32,2,28672]{2,1,0:T(2,128)(2,1)}), bf16[32,2,28672]{2,1,0:T(2,128)(2,1)}, u32[]{:S(2)}, u32[]{:S(2)}) async-start(bf16[32,2,28672]{2,1,0:T(2,128)(2,1)} %reshape.422), calls=%async_computation.1 | async-start | bytes 7340032 | tf_op jit(solution)/shard_map/all_to_all | solution.py:15
  198.3 20.6 %copy-start.1 = (s32[56,4]{0,1:T(4,128)S(1)}, s32[56,4]{0,1:T(4,128)}, u32[]{:S(2)}) copy-start(s32[56,4]{0,1:T(4,128)} %param.5) | copy-start | bytes 2692
  207.0 11.4 %all-to-all-start.2 = ((bf16[8,2,3584]{2,1,0:T(2,128)(2,1)}), bf16[8,2,3584]{2,1,0:T(2,128)(2,1)S(1)}, u32[]{:S(2)}, u32[]{:S(2)}) async-start(bf16[8,2,3584]{2,1,0:T(2,128)(2,1)} %reshape.424), calls=%async_computation.2 | async-start | bytes 229376 | tf_op jit(solution)/shard_map/all_to_all | solution.py:69
  210.4 107.9 %all-gather.3.cloned.1.call-start = ((), (), s32[]{:S(2)}) async-start(), calls=%async_computation.10 | async-start | bytes 15138816 | tf_op jit(solution)/shard_map/all_gather | solution.py:76
  232.4 417.4 %all-gather.5.cloned.1.call-start = ((), (), s32[]{:S(2)}) async-start(), calls=%async_computation.11 | async-start | bytes 15138816 | tf_op jit(solution)/shard_map/all_gather | solution.py:76
  318.3 31.1 %copy-start = (f32[56,4,256]{2,1,0:T(4,128)S(1)}, f32[56,4,256]{2,1,0:T(4,128)}, u32[]{:S(2)}) copy-start(f32[56,4,256]{2,1,0:T(4,128)} %param.4) | copy-start | bytes 688132
  666.2 14.8 %all-to-all-start.9 = ((bf16[8,2,3584]{2,1,0:T(2,128)(2,1)}), bf16[8,2,3584]{2,1,0:T(2,128)(2,1)S(1)}, u32[]{:S(2)}, u32[]{:S(2)}) async-start(bf16[8,2,3584]{2,1,0:T(2,128)(2,1)} %reshape.438), calls=%async_computation.9 | async-start | bytes 229376 | tf_op jit(solution)/shard_map/all_to_all | solution.py:78
Sparse Core Ops, SparseCore 0:
  232.6 85.6 all-gather.2
  564.1 85.6 all-gather.4
